TPU v7x, 32 devices: a whole 2x2x4 slice. The times are simulated.
32 devices in a mesh: dp: 4 (over y, x), vocab: 8 (over z, core).
Axes of the slice: x: 2, y: 2, z: 4, core: 2. Of those that a mesh axis runs over, the one named last changes fastest.
Arguments:
- hidden: bfloat16 [512, 8192], P('dp', 'vocab'), may hold values from -20 to 20
- weight: bfloat16 [8192, 4752], P('dp', 'vocab'), may hold values from -0.198873782 to 0.198873782
- targets: int32 [512], P('dp'), may hold values from 0 to 4751
- loss_mask: int32 [512], P('dp'), may hold values 0 or 1
Outputs:
- grad_hidden: bfloat16 [512, 8192], P('dp', 'vocab')
- grad_weight: bfloat16 [8192, 4752], P('dp', 'vocab')
- token_loss: float32 [512], P('dp')
- grad_norm: float32 [], replicated
All inputs are finite; a program needn't handle non-finite values. No bound on the sum of `loss_mask` on one device may be relied on, other than what follows from the above.
Results may differ from a plain program's by a relative error of at most 0.0034.
Values may be sent and summed in bfloat16 or wider, within the bound.
A program may use at most 128 MiB of HBM per device.

v0:
```python
import jax
import jax.numpy as jnp
from jax import lax
from jax.sharding import PartitionSpec as P

loss_scale = 16.0


def on_device(hidden, weight, targets, loss_mask):
    shard_width = weight.shape[1]
    col_offset = lax.axis_index("vocab") * shard_width
    full_hidden = lax.all_gather(hidden, "vocab", axis=1, tiled=True)
    hidden_block = lax.all_to_all(full_hidden, "dp", split_axis=1, concat_axis=0, tiled=True)
    full_weight = lax.all_gather(weight, "dp", axis=0, tiled=True)
    logits = jnp.dot(full_hidden, full_weight, preferred_element_type=jnp.float32)
    row_targets, row_mask = (targets, loss_mask)
    local_col = row_targets - col_offset
    onehot = (lax.broadcasted_iota(jnp.int32, logits.shape, 1) == local_col[:, None]).astype(
        jnp.float32
    )
    target_local = jnp.sum(logits * onehot, axis=1)
    local_top = jnp.max(logits, axis=1)
    row_top = lax.pmax(local_top, "vocab")
    local_sum = jnp.sum(jnp.exp(logits - row_top[:, None]), axis=1)
    exp_sum, target_logit = lax.psum((local_sum, target_local), "vocab")
    log_total = row_top + jnp.log(exp_sum)
    row_keep = row_mask.astype(jnp.float32)
    loss_rows = row_keep * (log_total - target_logit)
    softmax = jnp.exp(logits - log_total[:, None])
    dlogits = (loss_scale * row_keep[:, None] * (softmax - onehot)).astype(jnp.bfloat16)
    dlog_all = lax.all_gather(dlogits, "dp", axis=0, tiled=True)
    hidden_terms = lax.dot_general(
        dlogits, full_weight, (((1,), (1,)), ((), ())), preferred_element_type=jnp.float32
    )
    hidden_grad_full = lax.psum_scatter(hidden_terms, "vocab", scatter_dimension=1, tiled=True)
    weight_grad_full = lax.dot_general(
        hidden_block, dlog_all, (((0,), (0,)), ((), ())), preferred_element_type=jnp.float32
    )
    local_squares = jnp.sum(weight_grad_full * weight_grad_full) + jnp.sum(
        hidden_grad_full * hidden_grad_full
    )
    squares_total = lax.psum(local_squares, ("dp", "vocab"))
    return (
        hidden_grad_full.astype(jnp.bfloat16),
        weight_grad_full.astype(jnp.bfloat16),
        loss_rows,
        jnp.sqrt(squares_total),
    )


def solution(mesh):
    placed = (P("dp", "vocab"), P("dp", "vocab"), P("dp"), P("dp"))
    return jax.shard_map(
        on_device,
        mesh=mesh,
        in_specs=placed,
        out_specs=(P("dp", "vocab"), P("dp", "vocab"), P("dp"), P()),
        check_vma=False,
    )
```

profile of v0, /device:TPU:12, one launch (start us, length us, event | category | flops | bytes accessed | tf_op | source)
XLA Modules:
  0.0 285.6 jit_solution(2477782353101069427)
XLA Ops:
  7.2 0.0 copy-start.2
  7.2 0.0 all-gather.3.cloned.1.call-start
  7.2 1.8 copy.8
  9.0 0.0 all-gather.3.cloned.1.call-update
  9.0 0.0 all-gather.5.cloned.1.call-start
  9.1 0.7 all-gather.5.cloned.1.call-update
  9.8 0.0 reduce-scatter.2.cloned.1.call-start
  9.8 0.0 copy-done.2
  9.9 0.0 copy-start.1
  9.9 30.6 %all-gather.3.cloned.1.call-done = bf16[128,8192]{0,1:T(8,128)(2,1)} async-done(((bf16[128,1024]{0,1:T(8,128)(2,1)}), bf16[128,8192]{0,1:T(8,128)(2,1)}) %all-gather.3.cloned.1.call-update) | async-done | bytes 2097168 | tf_op jit(solution)/shard_map/all_gather | solution.py:12
  40.4 100.8 %all-gather.5.cloned.1.call-done = bf16[8192,594]{0,1:T(8,128)(2,1)} async-done(((bf16[2048,594]{0,1:T(8,128)(2,1)}), bf16[8192,594]{0,1:T(8,128)(2,1)}) %all-gather.5.cloned.1.call-update) | async-done | bytes 9732112 | tf_op jit(solution)/shard_map/all_gather | solution.py:14
  141.2 6.2 %fusion = (f32[128]{0:T(128)S(1)}, f32[128,594]{0,1:T(8,128)S(1)}) fusion(bf16[128,8192]{0,1:T(8,128)(2,1)} %all-gather.3.cloned.1.call-done, bf16[8192,594]{0,1:T(8,128)(2,1)} %all-gather.5.cloned.1.call-done), kind=kOutput, calls=%fused_computation.11 | convolution fusion | flops 1245784192 | bytes 12133888 | tf_op jit(solution)/shard_map/dot_general | solution.py:15
  147.4 12.7 %pmax.7 = f32[128]{0:T(128)S(1)} all-reduce(f32[128]{0:T(128)S(1)} %get-tuple-element.15), channel_id=1, replica_groups=mesh['dp'=4,'vocab'=8] {'vocab'}, use_global_device_ids=true, to_apply=%region_1.0 | all-reduce | flops 128 | bytes 1024 | tf_op jit(solution)/shard_map/pmax | solution.py:23
  160.1 0.1 select_reduce_fusion
  160.2 13.6 %all-reduce = (f32[128]{0:T(128)S(1)}, f32[128]{0:T(128)S(1)}) all-reduce(f32[128]{0:T(128)S(1)} %get-tuple-element.5, f32[128]{0:T(128)S(1)} %get-tuple-element.4), channel_id=1, replica_groups=mesh['dp'=4,'vocab'=8] {'vocab'}, use_global_device_ids=true, to_apply=%region_3.0 | all-reduce | flops 256 | bytes 2048 | tf_op jit(solution)/shard_map/psum | solution.py:25
  173.8 0.0 copy-done.1
  173.8 0.5 subtract_multiply_fusion
  174.3 0.1 multiply_convert_fusion
  174.4 8.0 %fusion.1 = f32[128,8192]{1,0:T(8,128)} fusion(bf16[128,594]{0,1:T(8,128)(2,1)S(1)} %multiply_convert_fusion, bf16[8192,594]{0,1:T(8,128)(2,1)} %all-gather.5.cloned.1.call-done), kind=kOutput, calls=%fused_computation.12 | convolution fusion | flops 1245708288 | bytes 14078464 | tf_op jit(solution)/shard_map/dot_general | solution.py:32
  182.4 0.0 copy-start
  182.4 0.0 reduce-scatter.2.cloned.1.call-update
  182.4 1.6 copy-done
  184.0 28.4 %all_to_all.19 = bf16[128,4,2048]{0,2,1:T(8,128)(2,1)} all-to-all(bf16[128,4,2048]{0,2,1:T(8,128)(2,1)S(1)} %bitcast.11), channel_id=1, replica_groups=mesh['dp'=4,'vocab'=8] {'dp'}, dimensions={1} | all-to-all | bytes 4194304 | tf_op jit(solution)/shard_map/all_to_all | solution.py:13
  212.3 2.9 %copy.9 = bf16[4,128,2048]{2,1,0:T(8,128)(2,1)S(1)} copy(bf16[4,128,2048]{1,2,0:T(8,128)(2,1)} %bitcast.12) | data formatting | bytes 4194304 | tf_op jit(solution)/shard_map/all_to_all | solution.py:13
  215.3 10.0 %all_gather.11 = bf16[512,594]{0,1:T(8,128)(2,1)S(1)} all-gather(bf16[128,594]{0,1:T(8,128)(2,1)S(1)} %multiply_convert_fusion), channel_id=1, replica_groups=mesh['dp'=4,'vocab'=8] {'dp'}, dimensions={0}, use_global_device_ids=true | all-gather | bytes 760320 | tf_op jit(solution)/shard_map/all_gather | solution.py:31
  225.3 3.6 %multiply_reduce_fusion = (f32[]{:T(128)}, bf16[2048,594]{0,1:T(8,128)(2,1)}) fusion(bf16[512,594]{0,1:T(8,128)(2,1)S(1)} %all_gather.11, bf16[512,2048]{1,0:T(8,128)(2,1)S(1)} %bitcast.13), kind=kOutput, calls=%fused_computation | convolution fusion | flops 1249357824 | bytes 5138436 | tf_op jit(solution)/shard_map/dot_general | solution.py:36
  228.9 1.2 reduce-scatter.2.cloned.1.call-done
  230.1 2.6 multiply_reduce_fusion.1
  234.0 43.3 %psum.23 = f32[]{:T(128)} all-reduce(f32[]{:T(128)S(6)} %add.15), channel_id=1, replica_groups=mesh['dp'=4,'vocab'=8] {'dp','vocab'}, use_global_device_ids=true, to_apply=%region_9.0 | all-reduce | flops 1 | bytes 8 | tf_op jit(solution)/shard_map/psum | solution.py:42
  (1 shorter events, 0.0 us)
Async XLA Ops:
  7.2 2.7 copy-start.2
  7.2 33.3 %all-gather.3.cloned.1.call-start = ((), (), s32[]{:S(2)}) async-start(), calls=%async_computation.2 | async-start | bytes 2359296 | tf_op jit(solution)/shard_map/all_gather | solution.py:12
  9.0 132.2 %all-gather.5.cloned.1.call-start = ((), (), s32[]{:S(2)}) async-start(), calls=%async_computation.3 | async-start | bytes 12288000 | tf_op jit(solution)/shard_map/all_gather | solution.py:14
  9.8 220.3 %reduce-scatter.2.cloned.1.call-start = ((), (), s32[]{:S(2)}) async-start(), calls=%async_computation.4 | async-start | bytes 4718592 | tf_op jit(solution)/shard_map/reduce_scatter | solution.py:35
  9.9 163.9 %copy-start.1 = (s32[128]{0:T(128)S(1)}, s32[128]{0:T(128)}, u32[]{:S(2)}) copy-start(s32[128]{0:T(128)} %param.7) | copy-start | bytes 1540
  182.4 1.6 copy-start
Sparse Core Ops, SparseCore 0:
  10.2 30.2 all-gather.2
  42.3 98.8 all-gather.4
  182.5 47.5 reduce-scatter.1
where the time goes:
time: 286 us
  waiting for transfers between devices  133 us (47%)
  blocking collectives  108 us (38%)
  matrix products  17.8 us (6%)
  between operations  17 us (6%)
  local copies, waits for them, and re-layouts  6.31 us (2%)
  other arithmetic  3.29 us (1%)
    all_gather x1, waiting for transfers between devices, on_device(): full_weight = lax.all_gather(weight, 'dp', axis=0, tiled=True)  101 us
    psum x1, blocking collectives, on_device(): squares_total = lax.psum(local_squares, ('dp', 'vocab'))  43.3 us
    all_gather x1, waiting for transfers between devices, on_device(): full_hidden = lax.all_gather(hidden, 'vocab', axis=1, tiled=True)  30.6 us
    all_to_all x1, blocking collectives, on_device(): lax.all_to_all(full_hidden, 'dp', split_axis=1, concat_axis=0, tiled=True)  28.4 us
    psum x1, blocking collectives, on_device(): exp_sum, target_logit = lax.psum((local_sum, target_local), 'vocab')  13.6 us
    pmax x1, blocking collectives, on_device(): row_top = lax.pmax(local_top, 'vocab')  12.7 us
    all_gather x1, blocking collectives, on_device(): dlog_all = lax.all_gather(dlogits, 'dp', axis=0, tiled=True)  10 us
    dot_general x1, matrix products, on_device(): lax.dot_general(dlogits, full_weight, (((1,), (1,)), ((), ())), preferred...  8.01 us
  transfers between devices with their start and end apart: 3, of which 3 were waited for; matrix products, arithmetic and copies ran while one was open for 2% of the time, Pallas kernels for 0%

commit v1 on v0

--- a/solution.py
+++ b/solution.py
@@ -10,7 +10,20 @@
     shard_width = weight.shape[1]
     col_offset = lax.axis_index("vocab") * shard_width
     full_hidden = lax.all_gather(hidden, "vocab", axis=1, tiled=True)
-    hidden_block = lax.all_to_all(full_hidden, "dp", split_axis=1, concat_axis=0, tiled=True)
+    ways, here = (lax.axis_size("dp"), lax.axis_index("dp"))
+    width = full_hidden.shape[1] // ways
+    shape = list(full_hidden.shape)
+    shape[1] = width
+    height = shape[0]
+    shape[0] = height * ways
+    hidden_block = jnp.zeros(shape, full_hidden.dtype)
+    for mask in range(ways):
+        part = lax.dynamic_slice_in_dim(full_hidden, (here ^ mask) * width, width, axis=1)
+        if mask:
+            part = lax.ppermute(part, "dp", [(d, d ^ mask) for d in range(ways)])
+        hidden_block = lax.dynamic_update_slice_in_dim(
+            hidden_block, part, (here ^ mask) * height, axis=0
+        )
     full_weight = lax.all_gather(weight, "dp", axis=0, tiled=True)
     logits = jnp.dot(full_hidden, full_weight, preferred_element_type=jnp.float32)
     row_targets, row_mask = (targets, loss_mask)

time: 286 us -> 285 us (level)
  blocking collectives: 108 us -> 80.3 us
  waiting for transfers between devices: 133 us -> 155 us
  starting transfers between devices: 0.12 us -> 3.6 us
    all_to_all x1 -> x0, blocking collectives: 28.4 us -> none  [on_device(): lax.all_to_all(full_hidden, 'dp', split_axis=1, concat_axis=0, tiled=True)]
    ppermute x0 -> x3, waiting for transfers between devices: none -> 20 us  [on_device(): part = lax.ppermute(part, 'dp', [(d, d ^ mask) for d in range(ways)])]
    ppermute x0 -> x3, starting transfers between devices: none -> 3.49 us  [on_device(): part = lax.ppermute(part, 'dp', [(d, d ^ mask) for d in range(ways)])]
    all_to_all x1 -> x0, local copies, waits for them, and re-layouts: 2.94 us -> none  [on_device(): lax.all_to_all(full_hidden, 'dp', split_axis=1, concat_axis=0, tiled=True)]
  transfers between devices with their start and end apart: 3 -> 6, of which waited for: 3 -> 5; matrix products, arithmetic and copies ran while one was open for 2% -> 3% of each run, Pallas kernels for 0% -> 0%
where the time goes in v1:
time: 285 us
  waiting for transfers between devices  155 us (54%)
  blocking collectives  80.3 us (28%)
  matrix products  19.3 us (7%)
  between operations  16.9 us (6%)
  local copies, waits for them, and re-layouts  6.44 us (2%)
  starting transfers between devices  3.6 us (1%)
  other arithmetic  3.29 us (1%)
    all_gather x1, waiting for transfers between devices, on_device(): full_weight = lax.all_gather(weight, 'dp', axis=0, tiled=True)  101 us
    psum x1, blocking collectives, on_device(): squares_total = lax.psum(local_squares, ('dp', 'vocab'))  43.3 us
    all_gather x1, waiting for transfers between devices, on_device(): full_hidden = lax.all_gather(hidden, 'vocab', axis=1, tiled=True)  31.1 us
    ppermute x3, waiting for transfers between devices, on_device(): part = lax.ppermute(part, 'dp', [(d, d ^ mask) for d in range(ways)])  20 us
    psum x1, blocking collectives, on_device(): exp_sum, target_logit = lax.psum((local_sum, target_local), 'vocab')  13.6 us
    pmax x1, blocking collectives, on_device(): row_top = lax.pmax(local_top, 'vocab')  12.7 us
    all_gather x1, blocking collectives, on_device(): dlog_all = lax.all_gather(dlogits, 'dp', axis=0, tiled=True)  10.7 us
    dot_general x1, matrix products, on_device(): lax.dot_general(dlogits, full_weight, (((1,), (1,)), ((), ())), preferred...  8.01 us
  transfers between devices with their start and end apart: 6, of which 5 were waited for; matrix products, arithmetic and copies ran while one was open for 3% of the time, Pallas kernels for 0%

profile of v1, /device:TPU:12, one launch (start us, length us, event | category | flops | bytes accessed | tf_op | source)
XLA Modules:
  0.0 285.0 jit_solution(10459876607209172909)
XLA Ops:
  7.2 0.0 copy-start.3
  7.2 0.0 all-gather.3.cloned.1.call-start
  7.2 0.7 all-gather.3.cloned.1.call-update
  7.9 0.0 all-gather.5.cloned.1.call-start
  8.0 0.7 all-gather.5.cloned.1.call-update
  8.7 0.0 reduce-scatter.2.cloned.1.call-start
  8.7 0.0 copy-done.3
  8.7 0.0 copy-start.2
  8.7 31.1 %all-gather.3.cloned.1.call-done = bf16[128,8192]{1,0:T(8,128)(2,1)} async-done(((bf16[128,1024]{1,0:T(8,128)(2,1)}), bf16[128,8192]{1,0:T(8,128)(2,1)}) %all-gather.3.cloned.1.call-update) | async-done | bytes 2097168 | tf_op jit(solution)/shard_map/all_gather | solution.py:12
  39.9 100.8 %all-gather.5.cloned.1.call-done = bf16[8192,594]{0,1:T(8,128)(2,1)} async-done(((bf16[2048,594]{0,1:T(8,128)(2,1)}), bf16[8192,594]{0,1:T(8,128)(2,1)}) %all-gather.5.cloned.1.call-update) | async-done | bytes 9732112 | tf_op jit(solution)/shard_map/all_gather | solution.py:27
  140.6 6.2 %fusion = (f32[128]{0:T(128)S(1)}, f32[128,594]{0,1:T(8,128)S(1)}) fusion(bf16[128,8192]{1,0:T(8,128)(2,1)} %all-gather.3.cloned.1.call-done, bf16[8192,594]{0,1:T(8,128)(2,1)} %all-gather.5.cloned.1.call-done), kind=kOutput, calls=%fused_computation.17 | convolution fusion | flops 1245784192 | bytes 12133888 | tf_op jit(solution)/shard_map/dot_general | solution.py:28
  146.8 12.7 %pmax.7 = f32[128]{0:T(128)S(1)} all-reduce(f32[128]{0:T(128)S(1)} %get-tuple-element.19), channel_id=1, replica_groups=mesh['dp'=4,'vocab'=8] {'vocab'}, use_global_device_ids=true, to_apply=%region_1.0 | all-reduce | flops 128 | bytes 1024 | tf_op jit(solution)/shard_map/pmax | solution.py:36
  159.5 0.1 select_reduce_fusion
  159.6 13.6 %all-reduce = (f32[128]{0:T(128)S(1)}, f32[128]{0:T(128)S(1)}) all-reduce(f32[128]{0:T(128)S(1)} %get-tuple-element.5, f32[128]{0:T(128)S(1)} %get-tuple-element.4), channel_id=1, replica_groups=mesh['dp'=4,'vocab'=8] {'vocab'}, use_global_device_ids=true, to_apply=%region_3.0 | all-reduce | flops 256 | bytes 2048 | tf_op jit(solution)/shard_map/psum | solution.py:38
  173.2 0.0 copy-done.2
  173.2 0.5 subtract_multiply_fusion
  173.7 0.1 multiply_convert_fusion
  173.8 8.0 %fusion.1 = f32[128,8192]{1,0:T(8,128)} fusion(bf16[128,594]{0,1:T(8,128)(2,1)S(1)} %multiply_convert_fusion, bf16[8192,594]{0,1:T(8,128)(2,1)} %all-gather.5.cloned.1.call-done), kind=kOutput, calls=%fused_computation.18 | convolution fusion | flops 1245708288 | bytes 14078464 | tf_op jit(solution)/shard_map/dot_general | solution.py:45
  181.9 0.0 reduce-scatter.2.cloned.1.call-update
  181.9 0.0 copy-start
  181.9 0.2 broadcast_in_dim.2
  182.2 1.3 copy-done
  183.5 1.0 constant_dynamic-slice_fusion
  184.5 0.0 copy-start.1
  184.5 1.3 copy-done.1
  185.8 0.6 collective-permute-start
  186.4 1.5 collective-permute-start.1
  187.9 1.5 collective-permute-start.2
  189.3 11.5 %collective-permute-done = bf16[128,2048]{1,0:T(8,128)(2,1)S(1)} collective-permute-done((bf16[128,2048]{1,0:T(8,128)(2,1)}, bf16[128,2048]{1,0:T(8,128)(2,1)S(1)}, u32[]{:S(2)}, u32[]{:S(2)}) %collective-permute-start) | collective-permute-done | bytes 524320 | tf_op jit(solution)/shard_map/ppermute | solution.py:23
  200.8 0.8 constant_dynamic-update-slice_fusion.1
  201.7 0.0 collective-permute-done.1
  201.7 0.8 constant_dynamic-update-slice_fusion
  202.5 8.5 %collective-permute-done.2 = bf16[128,2048]{1,0:T(8,128)(2,1)S(1)} collective-permute-done((bf16[128,2048]{1,0:T(8,128)(2,1)S(1)}, bf16[128,2048]{1,0:T(8,128)(2,1)S(1)}, u32[]{:S(2)}, u32[]{:S(2)}) %collective-permute-start.2) | collective-permute-done | bytes 524320 | tf_op jit(solution)/shard_map/ppermute | solution.py:23
  211.0 0.8 constant_dynamic-update-slice_fusion.2
  211.9 10.7 %all_gather.11 = bf16[512,594]{0,1:T(8,128)(2,1)S(1)} all-gather(bf16[128,594]{0,1:T(8,128)(2,1)S(1)} %multiply_convert_fusion), channel_id=1, replica_groups=mesh['dp'=4,'vocab'=8] {'dp'}, dimensions={0}, use_global_device_ids=true | all-gather | bytes 760320 | tf_op jit(solution)/shard_map/all_gather | solution.py:44
  222.6 5.1 %multiply_reduce_fusion = (f32[]{:T(128)}, bf16[2048,594]{0,1:T(8,128)(2,1)}) fusion(bf16[512,2048]{1,0:T(8,128)(2,1)} %constant_dynamic-update-slice_fusion.2, bf16[512,594]{0,1:T(8,128)(2,1)S(1)} %all_gather.11), kind=kOutput, calls=%fused_computation | convolution fusion | flops 1249357824 | bytes 5138436 | tf_op jit(solution)/shard_map/dot_general | solution.py:49
  227.7 1.9 reduce-scatter.2.cloned.1.call-done
  229.6 2.6 multiply_reduce_fusion.1
  233.4 43.3 %psum.23 = f32[]{:T(128)} all-reduce(f32[]{:T(128)S(6)} %add.47), channel_id=1, replica_groups=mesh['dp'=4,'vocab'=8] {'dp','vocab'}, use_global_device_ids=true, to_apply=%region_9.0 | all-reduce | flops 1 | bytes 8 | tf_op jit(solution)/shard_map/psum | solution.py:55
  (1 shorter events, 0.0 us)
Async XLA Ops:
  7.2 1.5 copy-start.3
  7.2 32.7 %all-gather.3.cloned.1.call-start = ((), (), s32[]{:S(2)}) async-start(), calls=%async_computation.1 | async-start | bytes 2359296 | tf_op jit(solution)/shard_map/all_gather | solution.py:12
  7.9 132.7 %all-gather.5.cloned.1.call-start = ((), (), s32[]{:S(2)}) async-start(), calls=%async_computation.2 | async-start | bytes 12288000 | tf_op jit(solution)/shard_map/all_gather | solution.py:27
  8.7 220.9 %reduce-scatter.2.cloned.1.call-start = ((), (), s32[]{:S(2)}) async-start(), calls=%async_computation.3 | async-start | bytes 4718592 | tf_op jit(solution)/shard_map/reduce_scatter | solution.py:48
  8.7 164.5 %copy-start.2 = (s32[128]{0:T(128)S(1)}, s32[128]{0:T(128)}, u32[]{:S(2)}) copy-start(s32[128]{0:T(128)} %param.7) | copy-start | bytes 1540
  181.9 1.6 copy-start
  184.5 1.4 copy-start.1
  185.8 15.0 %collective-permute-start = (bf16[128,2048]{1,0:T(8,128)(2,1)}, bf16[128,2048]{1,0:T(8,128)(2,1)S(1)}, u32[]{:S(2)}, u32[]{:S(2)}) collective-permute-start(bf16[128,2048]{1,0:T(8,128)(2,1)} %get-tuple-element.14), channel_id=1, source_target_pairs={{0,8},{8,0},{16,24},{24,16},{1,9},{9,1},{17,25},{25,17},{2,10},{10... | collective-permute-start | bytes 1572872 | tf_op jit(solution)/shard_map/ppermute | solution.py:23
  186.4 15.3 %collective-permute-start.1 = (bf16[128,2048]{1,0:T(8,128)(2,1)S(1)}, bf16[128,2048]{1,0:T(8,128)(2,1)S(1)}, u32[]{:S(2)}, u32[]{:S(2)}) collective-permute-start(bf16[128,2048]{1,0:T(8,128)(2,1)S(1)} %get-tuple-element.13), channel_id=1, source_target_pairs={{0,16},{8,24},{16,0},{24,8},{1,17},{9,25},{17,1},{25,9},{2,18},{10... | collective-permute-start | bytes 1572872 | tf_op jit(solution)/shard_map/ppermute | solution.py:23
  187.9 23.2 %collective-permute-start.2 = (bf16[128,2048]{1,0:T(8,128)(2,1)S(1)}, bf16[128,2048]{1,0:T(8,128)(2,1)S(1)}, u32[]{:S(2)}, u32[]{:S(2)}) collective-permute-start(bf16[128,2048]{1,0:T(8,128)(2,1)S(1)} %get-tuple-element.12), channel_id=1, source_target_pairs={{0,24},{8,16},{16,8},{24,0},{1,25},{9,17},{17,9},{25,1},{2,26},{10... | collective-permute-start | bytes 1572872 | tf_op jit(solution)/shard_map/ppermute | solution.py:23
Sparse Core Ops, SparseCore 0:
  9.6 30.2 all-gather.2
  41.7 98.8 all-gather.4
  182.0 47.5 reduce-scatter.1
